TPU v7x, 32 devices: a whole 2x2x4 slice. The times are simulated.
32 devices in a mesh: row: 4 (over z), col: 8 (over y, x, core).
Axes of the slice: x: 2, y: 2, z: 4, core: 2. Of those that a mesh axis runs over, the one named last changes fastest.
Arguments:
- minus_gradient: float32 [6, 16384], P(None, ('row', 'col')), may hold values from -10 to 10
- diag_blocks: float32 [36, 16384], P(None, ('row', 'col')), may hold values from -1000 to 1000, as said below
- hess_blocks: float32 [4, 8, 36, 4096], P('row', 'col'), may hold values from -40 to 40, as said below
- block_rows: int32 [4, 8, 4096], P('row', 'col'), may hold values from 0 to 2047
- block_cols: int32 [4, 8, 4096], P('row', 'col'), may hold values from 0 to 4095
- block_counts: int32 [4, 8], P('row', 'col'), may hold values from 0 to 4096, as said below
Outputs:
- pose_update: float32 [6, 16384], P(None, ('row', 'col'))
- residual: float32 [6, 16384], P(None, ('row', 'col'))
Inputs may be any that keep to these rules, and one draw needn't show every extreme that they name: `hess_blocks`: the live blocks of all tiles together with diag_blocks form a symmetric positive definite matrix; no live block lies on the diagonal; the slots after the live ones hold arbitrary entries. `diag_blocks`: each 6x6 block is symmetric positive definite. The live slots of a tile are its first block_counts slots.
All inputs are finite; a program needn't handle non-finite values.
Results may differ from a plain program's by a relative error of at most 0.0003.
Values sent between devices are 32-bit elements; how exact they have to be, the bound alone decides.
No kernel may reach another device: no remote copies, remote signals or barrier semaphores. Data moves between devices by JAX's collectives and lax.ppermute only.
A program may use at most 64 MiB of HBM per device.

v0:
```python
import math
import jax
import jax.numpy as jnp
from jax import lax
from jax.sharding import PartitionSpec as P

ITERS = 3


def factor_blocks(blocks):
    lower_part = {}
    reciprocals = []
    for j in range(6):
        pivot_value = blocks[7 * j]
        for k in range(j):
            pivot_value = pivot_value - lower_part[j, k] * lower_part[j, k]
        reciprocal = 1.0 / jnp.sqrt(pivot_value)
        reciprocals.append(reciprocal)
        for i in range(j + 1, 6):
            entry_value = blocks[6 * i + j]
            for k in range(j):
                entry_value = entry_value - lower_part[i, k] * lower_part[j, k]
            lower_part[i, j] = entry_value * reciprocal
    return (lower_part, reciprocals)


def apply_inverse(lower_part, reciprocals, vector):
    forward = []
    for i in range(6):
        running = vector[i]
        for k in range(i):
            running = running - lower_part[i, k] * forward[k]
        forward.append(running * reciprocals[i])
    backward = [None] * 6
    for i in range(5, -1, -1):
        running = forward[i]
        for k in range(i + 1, 6):
            running = running - lower_part[k, i] * backward[k]
        backward[i] = running * reciprocals[i]
    return jnp.stack(backward)


def diagonal_term(diag_blocks, vector):
    return jnp.sum(diag_blocks.reshape(6, 6, -1) * vector[None], axis=1)


def pick_columns(source, offsets):
    width = source.shape[1]
    low_width = math.gcd(128, width)
    high_width = width // low_width
    table = source.reshape(6 * high_width, low_width)
    slot_count = offsets.shape[0]
    block_size = math.gcd(512, slot_count)
    turns = slot_count // block_size

    def pick_one_block(carry, offset):
        low_part = offset % low_width
        high_part = offset // low_width
        low_onehot = (
            lax.broadcasted_iota(jnp.int32, (low_width, block_size), 0) == low_part[None, :]
        ).astype(jnp.float32)
        spread = jnp.dot(
            table, low_onehot, precision=lax.Precision.HIGHEST, preferred_element_type=jnp.float32
        )
        high_onehot = (
            lax.broadcasted_iota(jnp.int32, (high_width, block_size), 0) == high_part[None, :]
        ).astype(jnp.float32)
        chosen = jnp.sum(spread.reshape(6, high_width, block_size) * high_onehot[None], axis=1)
        return (carry, chosen)

    unused, blocks_out = lax.scan(pick_one_block, None, offsets.reshape(turns, block_size))
    return jnp.transpose(blocks_out, (1, 0, 2)).reshape(6, slot_count)


def add_rows(terms, rows, span_size):
    low_width = math.gcd(128, span_size)
    high_width = span_size // low_width
    slot_count = rows.shape[0]
    block_size = math.gcd(512, slot_count)
    turns = slot_count // block_size
    term_blocks = jnp.transpose(terms.reshape(6, turns, block_size), (1, 0, 2))
    row_blocks = rows.reshape(turns, block_size)

    def add_one_block(carry, inputs):
        term_block, row_block = inputs
        high_onehot = (
            lax.broadcasted_iota(jnp.int32, (high_width, block_size), 0)
            == (row_block // low_width)[None, :]
        ).astype(jnp.float32)
        spread = (term_block[:, None, :] * high_onehot[None]).reshape(6 * high_width, block_size)
        low_onehot = (
            (row_block % low_width)[:, None]
            == lax.broadcasted_iota(jnp.int32, (block_size, low_width), 1)
        ).astype(jnp.float32)
        carry = carry + jnp.dot(
            spread, low_onehot, precision=lax.Precision.HIGHEST, preferred_element_type=jnp.float32
        )
        return (carry, None)

    start_total = jnp.zeros((6 * high_width, low_width), jnp.float32)
    total, unused = lax.scan(add_one_block, start_total, (term_blocks, row_blocks))
    return total.reshape(6, span_size)


def merged_sums(residual, precond, hess_image):
    return lax.psum((jnp.sum(residual * precond), jnp.sum(hess_image * precond)), ("row", "col"))


def on_device(minus_gradient, diag_blocks, hess_blocks, block_rows, block_cols, block_counts):
    pose_dev = minus_gradient.shape[1]
    blocks = hess_blocks.reshape(6, 6, -1)
    local_rows = block_rows.reshape(-1)
    local_cols = block_cols.reshape(-1)
    slot_count = local_rows.shape[0]
    live_mask = jnp.arange(slot_count, dtype=jnp.int32) < block_counts.reshape(())
    span_size = pose_dev * lax.axis_size("row")
    lower_part, reciprocals = factor_blocks(diag_blocks)

    def tile_terms(picked):
        return jnp.sum(blocks * picked[None], axis=1)

    def hessian(vector):
        gathered = lax.all_gather(vector, "col", axis=1, tiled=True)
        picked = pick_columns(gathered, local_cols)
        live_terms = jnp.where(live_mask[None, :], tile_terms(picked), 0.0)
        partial_value = add_rows(live_terms, local_rows, span_size)
        own_term = diagonal_term(diag_blocks, vector)
        summed = lax.psum(partial_value, "row")
        reduced = lax.dynamic_slice_in_dim(summed, lax.axis_index("row") * pose_dev, pose_dev, 1)
        return reduced + own_term

    solution = jnp.zeros_like(minus_gradient)
    residual = minus_gradient
    precond = apply_inverse(lower_part, reciprocals, residual)
    hess_image = hessian(precond)
    rho_now, curv_value = merged_sums(residual, precond, hess_image)
    step_size = rho_now / curv_value
    direction = precond
    along_image = hess_image
    for k in range(ITERS):
        solution = solution + step_size * direction
        residual = residual - step_size * along_image
        if k + 1 < ITERS:
            precond = apply_inverse(lower_part, reciprocals, residual)
            hess_image = hessian(precond)
            rho_next, curv_value = merged_sums(residual, precond, hess_image)
            ratio_next = rho_next / rho_now
            step_size = rho_next / (curv_value - ratio_next * rho_next / step_size)
            direction = precond + ratio_next * direction
            along_image = hess_image + ratio_next * along_image
            rho_now = rho_next
    return (solution, residual)


def solution(mesh):
    placed = (
        P(None, ("row", "col")),
        P(None, ("row", "col")),
        P("row", "col", None, None),
        P("row", "col", None),
        P("row", "col", None),
        P("row", "col"),
    )
    return jax.shard_map(
        on_device,
        mesh=mesh,
        in_specs=placed,
        out_specs=(P(None, ("row", "col")), P(None, ("row", "col"))),
        check_vma=False,
    )
```

profile of v0, /device:TPU:14, one launch (start us, length us, event | category | flops | bytes accessed | tf_op | source)
XLA Modules:
  0.0 246.8 jit_solution(5160269623161957242)
XLA Ops:
  0.6 1.1 subtract_multiply_fusion.21
  1.7 0.7 copy-done.2
  2.6 8.2 %all_gather.9 = f32[6,4096]{1,0:T(8,128)S(1)} all-gather(f32[6,512]{1,0:T(8,128)S(1)} %stack.6), channel_id=1, replica_groups=mesh['row'=4,'col'=8] {'col'}, dimensions={1}, use_global_device_ids=true | all-gather | bytes 110592 | tf_op jit(solution)/shard_map/all_gather | solution.py:123
  10.9 0.5 broadcast.572
  11.5 0.7 reduce.7
  12.3 3.9 %while.75 = (s32[]{:T(128)}, f32[8,6,512]{2,1,0:T(8,128)S(1)}, s32[8,512]{1,0:T(8,128)S(1)}, f32[192,128]{1,0:T(8,128)S(1)}, s32[]{:T(128)}) while((s32[]{:T(128)}, f32[8,6,512]{2,1,0:T(8,128)S(1)}, s32[8,512]{1,0:T(8,128)S(1)}, f32[192,128]{1,0:T(8,128)S(1)}, s32[]{:T(128)}) %tuple.218), condition=%wide.region_4.5_spmd, body=%wide.region_2.4_spmd.sunk | while | flops 151297024 | bytes 1075269 | solution.py:71
  16.2 1.4 reduce
  18.7 0.7 copy-done.4
  19.4 0.7 reduce.8
  20.1 3.9 %while.78 = (s32[]{:T(128)}, f32[96,128]{1,0:T(8,128)S(1)}, f32[8,6,512]{2,1,0:T(8,128)S(1)}, s32[8,512]{1,0:T(8,128)S(1)}, s32[]{:T(128)}, /*index=5*/s32[]{:T(128)}) while((s32[]{:T(128)}, f32[96,128]{1,0:T(8,128)S(1)}, f32[8,6,512]{2,1,0:T(8,128)S(1)}, s32[8,512]{1,0:T(8,128)S(1)}, s32[]{:T(128)}, /*index=5*/s32[]{:T(128)}) %tuple.221), condition=%wide.region_7.8_spmd.clone, body=%wide.region_6.7_spmd.clone.sunk | while | flops 75666432 | bytes 608343 | solution.py:101
  21.6 0.4 convolution_add_fusion.6
  22.6 0.4 convolution_add_fusion.6
  23.6 0.4 convolution_add_fusion.6
  24.0 16.2 %psum.64 = f32[6,2048]{1,0:T(8,128)S(1)} all-reduce(f32[6,2048]{1,0:T(8,128)S(1)} %reshape.316), channel_id=1, replica_groups=mesh['row'=4,'col'=8] {'row'}, use_global_device_ids=true, to_apply=%region_8.9 | all-reduce | flops 12288 | bytes 98304 | tf_op jit(solution)/shard_map/psum | solution.py:128
  40.3 0.6 multiply_reduce_fusion.13
  40.9 44.0 %all-reduce.2 = (f32[]{:T(128)}, f32[]{:T(128)}) all-reduce(f32[]{:T(128)} %get-tuple-element.394, f32[]{:T(128)} %get-tuple-element.393), channel_id=1, replica_groups=mesh['row'=4,'col'=8] {'row','col'}, use_global_device_ids=true, to_apply=%region_1.2 | all-reduce | flops 2 | bytes 16 | tf_op jit(solution)/shard_map/psum | solution.py:106
  86.4 8.2 %all_gather.10 = f32[6,4096]{1,0:T(8,128)S(1)} all-gather(f32[6,512]{1,0:T(8,128)S(1)} %stack.7), channel_id=1, replica_groups=mesh['row'=4,'col'=8] {'col'}, dimensions={1}, use_global_device_ids=true | all-gather | bytes 110592 | tf_op jit(solution)/shard_map/all_gather | solution.py:123
  94.6 3.9 %while.76 = (s32[]{:T(128)}, f32[8,6,512]{2,1,0:T(8,128)S(1)}, s32[8,512]{1,0:T(8,128)S(1)}, f32[192,128]{1,0:T(8,128)S(1)}, s32[]{:T(128)}) while((s32[]{:T(128)}, f32[8,6,512]{2,1,0:T(8,128)S(1)}, s32[8,512]{1,0:T(8,128)S(1)}, f32[192,128]{1,0:T(8,128)S(1)}, s32[]{:T(128)}) %tuple.236), condition=%wide.region_16.17_spmd, body=%wide.region_14.16_spmd.sunk | while | flops 151297024 | bytes 1075269 | solution.py:71
  98.9 3.9 %while.79 = (s32[]{:T(128)}, f32[96,128]{1,0:T(8,128)S(1)}, f32[8,6,512]{2,1,0:T(8,128)S(1)}, s32[8,512]{1,0:T(8,128)S(1)}, s32[]{:T(128)}, /*index=5*/s32[]{:T(128)}) while((s32[]{:T(128)}, f32[96,128]{1,0:T(8,128)S(1)}, f32[8,6,512]{2,1,0:T(8,128)S(1)}, s32[8,512]{1,0:T(8,128)S(1)}, s32[]{:T(128)}, ...), condition=%wide.region_19.20_spmd.clone, body=%wide.region_18.19_spmd.clone.sunk | while | flops 75666432 | bytes 608343 | solution.py:101
  99.5 0.4 convolution_add_fusion.7
  100.5 0.4 convolution_add_fusion.7
  101.4 0.4 convolution_add_fusion.7
  102.8 14.3 %psum.67 = f32[6,2048]{1,0:T(8,128)S(1)} all-reduce(f32[6,2048]{1,0:T(8,128)S(1)} %reshape.319), channel_id=1, replica_groups=mesh['row'=4,'col'=8] {'row'}, use_global_device_ids=true, to_apply=%region_20.21 | all-reduce | flops 12288 | bytes 98304 | tf_op jit(solution)/shard_map/psum | solution.py:128
  117.1 0.7 multiply_reduce_fusion.11
  117.8 44.2 %all-reduce.1 = (f32[]{:T(128)}, f32[]{:T(128)}) all-reduce(f32[]{:T(128)} %get-tuple-element.392, f32[]{:T(128)} %get-tuple-element.391), channel_id=1, replica_groups=mesh['row'=4,'col'=8] {'row','col'}, use_global_device_ids=true, to_apply=%region_13.14 | all-reduce | flops 2 | bytes 16 | tf_op jit(solution)/shard_map/psum | solution.py:106
  166.7 8.1 %all_gather.11 = f32[6,4096]{1,0:T(8,128)S(1)} all-gather(f32[6,512]{1,0:T(8,128)S(1)} %stack.8), channel_id=1, replica_groups=mesh['row'=4,'col'=8] {'col'}, dimensions={1}, use_global_device_ids=true | all-gather | bytes 110592 | tf_op jit(solution)/shard_map/all_gather | solution.py:123
  174.9 3.9 %while.77 = (s32[]{:T(128)}, f32[8,6,512]{2,1,0:T(8,128)S(1)}, s32[8,512]{1,0:T(8,128)S(1)}, f32[192,128]{1,0:T(8,128)S(1)}, s32[]{:T(128)}) while((s32[]{:T(128)}, f32[8,6,512]{2,1,0:T(8,128)S(1)}, s32[8,512]{1,0:T(8,128)S(1)}, f32[192,128]{1,0:T(8,128)S(1)}, s32[]{:T(128)}) %tuple.237), condition=%wide.region_28.29_spmd, body=%wide.region_26.28_spmd.sunk | while | flops 151297024 | bytes 1075269 | solution.py:71
  179.1 3.9 %while.80 = (s32[]{:T(128)}, f32[96,128]{1,0:T(8,128)S(1)}, f32[8,6,512]{2,1,0:T(8,128)S(1)}, s32[8,512]{1,0:T(8,128)S(1)}, s32[]{:T(128)}, /*index=5*/s32[]{:T(128)}) while((s32[]{:T(128)}, f32[96,128]{1,0:T(8,128)S(1)}, f32[8,6,512]{2,1,0:T(8,128)S(1)}, s32[8,512]{1,0:T(8,128)S(1)}, s32[]{:T(128)}, ...), condition=%wide.region_31.32_spmd.clone, body=%wide.region_30.31_spmd.clone.sunk | while | flops 75666432 | bytes 608343 | solution.py:101
  183.0 14.4 %psum.70 = f32[6,2048]{1,0:T(8,128)S(1)} all-reduce(f32[6,2048]{1,0:T(8,128)S(1)} %reshape.321), channel_id=1, replica_groups=mesh['row'=4,'col'=8] {'row'}, use_global_device_ids=true, to_apply=%region_32.33 | all-reduce | flops 12288 | bytes 98304 | tf_op jit(solution)/shard_map/psum | solution.py:128
  197.5 0.6 multiply_reduce_fusion.9
  198.1 44.1 %all-reduce = (f32[]{:T(128)}, f32[]{:T(128)}) all-reduce(f32[]{:T(128)} %get-tuple-element.390, f32[]{:T(128)} %get-tuple-element.389), channel_id=1, replica_groups=mesh['row'=4,'col'=8] {'row','col'}, use_global_device_ids=true, to_apply=%region_25.26 | all-reduce | flops 2 | bytes 16 | tf_op jit(solution)/shard_map/psum | solution.py:106
  246.2 0.6 multiply_subtract_fusion
  (326 shorter events, 20.2 us)
Async XLA Ops:
  0.6 1.1 copy-start.1
  1.7 0.7 copy-start.2
  10.8 0.7 copy-start.3
  12.2 4.0 %copy-start = (f32[1,1,36,4096]{3,1,2,0:T(1,128)S(1)}, f32[1,1,36,4096]{3,1,2,0:T(1,128)}, u32[]{:S(2)}) copy-start(f32[1,1,36,4096]{3,1,2,0:T(1,128)} %param.20) | copy-start | bytes 1769476
  18.6 0.7 copy-start.4
where the time goes:
time: 248 us; the launch traced here: 247 us
  blocking collectives  202 us (81%)
  matrix products  16.6 us (7%)
  between operations  11.5 us (5%)
  other arithmetic  11.1 us (4%)
  loops' own time  2.93 us (1%)
  local copies, waits for them, and re-layouts  2.92 us (1%)
    psum x3, blocking collectives, merged_sums(): lax.psum((jnp.sum(residual * precond), jnp.sum(hess_image * precond)), ('...  132 us
    psum x3, blocking collectives, hessian(): summed = lax.psum(partial_value, 'row')  44.9 us
    all_gather x3, blocking collectives, hessian(): gathered = lax.all_gather(vector, 'col', axis=1, tiled=True)  24.5 us
    dot_general x24, matrix products, add_one_block(): jnp.dot(spread, low_onehot, precision=lax.Precision.HIGHEST, preferred_el...  8.61 us
    dot_general x24, matrix products, pick_one_block(): jnp.dot(table, low_onehot, precision=lax.Precision.HIGHEST, preferred_ele...  7.99 us

commit v1 on v0

--- a/solution.py
+++ b/solution.py
@@ -5,6 +5,19 @@
 from jax.sharding import PartitionSpec as P
 
 ITERS = 3
+
+
+def arrange_sample(v0, mesh_name):
+    n_peers_all = lax.axis_size(mesh_name)
+    a_now, answer = (v0, 0)
+    while 1 << answer < n_peers_all:
+        long_array = range(n_peers_all)
+        view_out = map(lambda to_i: (to_i, to_i ^ 1 << answer), long_array)
+        local_next = list(view_out)
+        oldest = lax.ppermute(a_now, mesh_name, local_next)
+        a_now = a_now + oldest
+        answer = answer + 1
+    return a_now
 
 
 def factor_blocks(blocks):
@@ -125,7 +138,7 @@
         live_terms = jnp.where(live_mask[None, :], tile_terms(picked), 0.0)
         partial_value = add_rows(live_terms, local_rows, span_size)
         own_term = diagonal_term(diag_blocks, vector)
-        summed = lax.psum(partial_value, "row")
+        summed = arrange_sample(partial_value, "row")
         reduced = lax.dynamic_slice_in_dim(summed, lax.axis_index("row") * pose_dev, pose_dev, 1)
         return reduced + own_term
 

time: 248 us -> 224 us (0.903)
  blocking collectives: 202 us -> 149 us
  waiting for transfers between devices: 0 us -> 20.6 us
  starting transfers between devices: 0 us -> 8.18 us
    psum x3 -> x0, blocking collectives: 44.9 us -> none  [hessian(): summed = lax.psum(partial_value, 'row')]
    ppermute x0 -> x6, waiting for transfers between devices: none -> 20.6 us  [arrange_sample(): oldest = lax.ppermute(a_now, mesh_name, local_next)]
    ppermute x0 -> x6, starting transfers between devices: none -> 8.18 us  [arrange_sample(): oldest = lax.ppermute(a_now, mesh_name, local_next)]
    psum x3, blocking collectives: 132 us -> 125 us  [merged_sums(): lax.psum((jnp.sum(residual * precond), jnp.sum(hess_image * precond)), ('...]
  transfers between devices with their start and end apart: 0 -> 6, of which waited for: 0 -> 6; matrix products, arithmetic and copies ran while one was open for 0% -> 0% of each run, Pallas kernels for 0% -> 0%
where the time goes in v1:
time: 224 us; the launch traced here: 223 us
  blocking collectives  149 us (67%)
  waiting for transfers between devices  20.6 us (9%)
  matrix products  16.6 us (7%)
  between operations  11.8 us (5%)
  other arithmetic  11.2 us (5%)
  starting transfers between devices  8.18 us (4%)
  loops' own time  2.91 us (1%)
  local copies, waits for them, and re-layouts  2.25 us (1%)
    psum x3, blocking collectives, merged_sums(): lax.psum((jnp.sum(residual * precond), jnp.sum(hess_image * precond)), ('...  125 us
    all_gather x3, blocking collectives, hessian(): gathered = lax.all_gather(vector, 'col', axis=1, tiled=True)  24.6 us
    ppermute x6, waiting for transfers between devices, arrange_sample(): oldest = lax.ppermute(a_now, mesh_name, local_next)  20.6 us
    dot_general x24, matrix products, add_one_block(): jnp.dot(spread, low_onehot, precision=lax.Precision.HIGHEST, preferred_el...  8.61 us
    ppermute x6, starting transfers between devices, arrange_sample(): oldest = lax.ppermute(a_now, mesh_name, local_next)  8.18 us
    dot_general x24, matrix products, pick_one_block(): jnp.dot(table, low_onehot, precision=lax.Precision.HIGHEST, preferred_ele...  7.98 us
  transfers between devices with their start and end apart: 6, of which 6 were waited for; matrix products, arithmetic and copies ran while one was open for 0% of the time, Pallas kernels for 0%

profile of v1, /device:TPU:14, one launch (start us, length us, event | category | flops | bytes accessed | tf_op | source)
XLA Modules:
  0.0 223.0 jit_solution(15816408749644590172)
XLA Ops:
  0.7 1.1 subtract_multiply_fusion.21
  1.8 0.7 copy-done.2
  2.6 8.2 %all_gather.9 = f32[6,4096]{1,0:T(8,128)S(1)} all-gather(f32[6,512]{1,0:T(8,128)S(1)} %stack.6), channel_id=1, replica_groups=mesh['row'=4,'col'=8] {'col'}, dimensions={1}, use_global_device_ids=true | all-gather | bytes 110592 | tf_op jit(solution)/shard_map/all_gather | solution.py:136
  10.9 0.6 broadcast.572
  11.5 0.7 reduce.7
  12.3 3.9 %while.75 = (s32[]{:T(128)}, f32[8,6,512]{2,1,0:T(8,128)S(1)}, s32[8,512]{1,0:T(8,128)S(1)}, f32[192,128]{1,0:T(8,128)S(1)}, s32[]{:T(128)}) while((s32[]{:T(128)}, f32[8,6,512]{2,1,0:T(8,128)S(1)}, s32[8,512]{1,0:T(8,128)S(1)}, f32[192,128]{1,0:T(8,128)S(1)}, s32[]{:T(128)}) %tuple.219), condition=%wide.region_4.5_spmd, body=%wide.region_2.4_spmd.sunk | while | flops 151297024 | bytes 1075269 | solution.py:84
  16.2 1.4 reduce
  18.4 0.7 reduce.8
  19.5 3.9 %while.78 = (s32[]{:T(128)}, f32[96,128]{1,0:T(8,128)S(1)}, f32[8,6,512]{2,1,0:T(8,128)S(1)}, s32[8,512]{1,0:T(8,128)S(1)}, s32[]{:T(128)}, /*index=5*/s32[]{:T(128)}) while((s32[]{:T(128)}, f32[96,128]{1,0:T(8,128)S(1)}, f32[8,6,512]{2,1,0:T(8,128)S(1)}, s32[8,512]{1,0:T(8,128)S(1)}, s32[]{:T(128)}, /*index=5*/s32[]{:T(128)}) %tuple.222), condition=%wide.region_7.8_spmd.clone, body=%wide.region_6.7_spmd.clone.sunk | while | flops 75666432 | bytes 608343 | solution.py:114
  23.9 3.9 %collective-permute-done = f32[6,2048]{1,0:T(8,128)S(1)} collective-permute-done((f32[6,2048]{1,0:T(8,128)S(1)}, f32[6,2048]{1,0:T(8,128)S(1)}, u32[]{:S(2)}, u32[]{:S(2)}) %collective-permute-start) | collective-permute-done | bytes 49184 | tf_op jit(solution)/shard_map/ppermute | solution.py:17
  27.8 2.7 %collective-permute-start.1 = (f32[6,2048]{1,0:T(8,128)S(1)}, f32[6,2048]{1,0:T(8,128)S(1)}, u32[]{:S(2)}, u32[]{:S(2)}) collective-permute-start(f32[6,2048]{1,0:T(8,128)S(1)} %add.206), channel_id=1, source_target_pairs={{0,16},{8,24},{16,0},{24,8},{1,17},{9,25},{17,1},{25,9},{2,18},{10... | collective-permute-start | bytes 147464 | tf_op jit(solution)/shard_map/ppermute | solution.py:17
  30.5 2.5 %collective-permute-done.1 = f32[6,2048]{1,0:T(8,128)S(1)} collective-permute-done((f32[6,2048]{1,0:T(8,128)S(1)}, f32[6,2048]{1,0:T(8,128)S(1)}, u32[]{:S(2)}, u32[]{:S(2)}) %collective-permute-start.1) | collective-permute-done | bytes 49184 | tf_op jit(solution)/shard_map/ppermute | solution.py:17
  33.0 0.6 multiply_reduce_fusion.13
  33.6 42.2 %all-reduce.2 = (f32[]{:T(128)}, f32[]{:T(128)}) all-reduce(f32[]{:T(128)} %get-tuple-element.394, f32[]{:T(128)} %get-tuple-element.393), channel_id=1, replica_groups=mesh['row'=4,'col'=8] {'row','col'}, use_global_device_ids=true, to_apply=%region_1.2 | all-reduce | flops 2 | bytes 16 | tf_op jit(solution)/shard_map/psum | solution.py:119
  77.4 8.2 %all_gather.10 = f32[6,4096]{1,0:T(8,128)S(1)} all-gather(f32[6,512]{1,0:T(8,128)S(1)} %stack.7), channel_id=1, replica_groups=mesh['row'=4,'col'=8] {'col'}, dimensions={1}, use_global_device_ids=true | all-gather | bytes 110592 | tf_op jit(solution)/shard_map/all_gather | solution.py:136
  85.7 3.9 %while.76 = (s32[]{:T(128)}, f32[8,6,512]{2,1,0:T(8,128)S(1)}, s32[8,512]{1,0:T(8,128)S(1)}, f32[192,128]{1,0:T(8,128)S(1)}, s32[]{:T(128)}) while((s32[]{:T(128)}, f32[8,6,512]{2,1,0:T(8,128)S(1)}, s32[8,512]{1,0:T(8,128)S(1)}, f32[192,128]{1,0:T(8,128)S(1)}, s32[]{:T(128)}) %tuple.239), condition=%wide.region_15.16_spmd, body=%wide.region_13.15_spmd.sunk | while | flops 151297024 | bytes 1075269 | solution.py:84
  89.9 3.9 %while.79 = (s32[]{:T(128)}, f32[96,128]{1,0:T(8,128)S(1)}, f32[8,6,512]{2,1,0:T(8,128)S(1)}, s32[8,512]{1,0:T(8,128)S(1)}, s32[]{:T(128)}, /*index=5*/s32[]{:T(128)}) while((s32[]{:T(128)}, f32[96,128]{1,0:T(8,128)S(1)}, f32[8,6,512]{2,1,0:T(8,128)S(1)}, s32[8,512]{1,0:T(8,128)S(1)}, s32[]{:T(128)}, ...), condition=%wide.region_18.19_spmd.clone, body=%wide.region_17.18_spmd.clone.sunk | while | flops 75666432 | bytes 608343 | solution.py:114
  93.9 4.3 %collective-permute-done.2 = f32[6,2048]{1,0:T(8,128)S(1)} collective-permute-done((f32[6,2048]{1,0:T(8,128)S(1)}, f32[6,2048]{1,0:T(8,128)S(1)}, u32[]{:S(2)}, u32[]{:S(2)}) %collective-permute-start.2) | collective-permute-done | bytes 49184 | tf_op jit(solution)/shard_map/ppermute | solution.py:17
  98.2 1.2 collective-permute-start.3
  99.4 4.0 %collective-permute-done.3 = f32[6,2048]{1,0:T(8,128)S(1)} collective-permute-done((f32[6,2048]{1,0:T(8,128)S(1)}, f32[6,2048]{1,0:T(8,128)S(1)}, u32[]{:S(2)}, u32[]{:S(2)}) %collective-permute-start.3) | collective-permute-done | bytes 49184 | tf_op jit(solution)/shard_map/ppermute | solution.py:17
  103.4 0.7 multiply_reduce_fusion.11
  104.1 40.6 %all-reduce.1 = (f32[]{:T(128)}, f32[]{:T(128)}) all-reduce(f32[]{:T(128)} %get-tuple-element.392, f32[]{:T(128)} %get-tuple-element.391), channel_id=1, replica_groups=mesh['row'=4,'col'=8] {'row','col'}, use_global_device_ids=true, to_apply=%region_12.13 | all-reduce | flops 2 | bytes 16 | tf_op jit(solution)/shard_map/psum | solution.py:119
  149.6 8.2 %all_gather.11 = f32[6,4096]{1,0:T(8,128)S(1)} all-gather(f32[6,512]{1,0:T(8,128)S(1)} %stack.8), channel_id=1, replica_groups=mesh['row'=4,'col'=8] {'col'}, dimensions={1}, use_global_device_ids=true | all-gather | bytes 110592 | tf_op jit(solution)/shard_map/all_gather | solution.py:136
  157.9 3.9 %while.77 = (s32[]{:T(128)}, f32[8,6,512]{2,1,0:T(8,128)S(1)}, s32[8,512]{1,0:T(8,128)S(1)}, f32[192,128]{1,0:T(8,128)S(1)}, s32[]{:T(128)}) while((s32[]{:T(128)}, f32[8,6,512]{2,1,0:T(8,128)S(1)}, s32[8,512]{1,0:T(8,128)S(1)}, f32[192,128]{1,0:T(8,128)S(1)}, s32[]{:T(128)}) %tuple.240), condition=%wide.region_26.27_spmd, body=%wide.region_24.26_spmd.sunk | while | flops 151297024 | bytes 1075269 | solution.py:84
  162.1 3.9 %while.80 = (s32[]{:T(128)}, f32[96,128]{1,0:T(8,128)S(1)}, f32[8,6,512]{2,1,0:T(8,128)S(1)}, s32[8,512]{1,0:T(8,128)S(1)}, s32[]{:T(128)}, /*index=5*/s32[]{:T(128)}) while((s32[]{:T(128)}, f32[96,128]{1,0:T(8,128)S(1)}, f32[8,6,512]{2,1,0:T(8,128)S(1)}, s32[8,512]{1,0:T(8,128)S(1)}, s32[]{:T(128)}, ...), condition=%wide.region_29.30_spmd.clone, body=%wide.region_28.29_spmd.clone.sunk | while | flops 75666432 | bytes 608343 | solution.py:114
  166.0 1.6 collective-permute-start.4
  167.6 2.8 %collective-permute-done.4 = f32[6,2048]{1,0:T(8,128)S(1)} collective-permute-done((f32[6,2048]{1,0:T(8,128)S(1)}, f32[6,2048]{1,0:T(8,128)S(1)}, u32[]{:S(2)}, u32[]{:S(2)}) %collective-permute-start.4) | collective-permute-done | bytes 49184 | tf_op jit(solution)/shard_map/ppermute | solution.py:17
  170.5 2.2 collective-permute-start.5
  172.7 3.0 %collective-permute-done.5 = f32[6,2048]{1,0:T(8,128)S(1)} collective-permute-done((f32[6,2048]{1,0:T(8,128)S(1)}, f32[6,2048]{1,0:T(8,128)S(1)}, u32[]{:S(2)}, u32[]{:S(2)}) %collective-permute-start.5) | collective-permute-done | bytes 49184 | tf_op jit(solution)/shard_map/ppermute | solution.py:17
  175.8 0.6 multiply_reduce_fusion.9
  176.4 42.0 %all-reduce = (f32[]{:T(128)}, f32[]{:T(128)}) all-reduce(f32[]{:T(128)} %get-tuple-element.390, f32[]{:T(128)} %get-tuple-element.389), channel_id=1, replica_groups=mesh['row'=4,'col'=8] {'row','col'}, use_global_device_ids=true, to_apply=%region_23.24 | all-reduce | flops 2 | bytes 16 | tf_op jit(solution)/shard_map/psum | solution.py:119
  222.4 0.6 multiply_subtract_fusion
  (338 shorter events, 22.9 us)
Async XLA Ops:
  0.6 1.1 copy-start.1
  1.7 0.7 copy-start.2
  10.8 0.7 copy-start.3
  12.3 3.9 %copy-start = (f32[1,1,36,4096]{3,1,2,0:T(1,128)S(1)}, f32[1,1,36,4096]{3,1,2,0:T(1,128)}, u32[]{:S(2)}) copy-start(f32[1,1,36,4096]{3,1,2,0:T(1,128)} %param.20) | copy-start | bytes 1769476
  17.7 0.8 copy-start.4
  23.4 4.4 %collective-permute-start = (f32[6,2048]{1,0:T(8,128)S(1)}, f32[6,2048]{1,0:T(8,128)S(1)}, u32[]{:S(2)}, u32[]{:S(2)}) collective-permute-start(f32[6,2048]{1,0:T(8,128)S(1)} %reshape.316), channel_id=1, source_target_pairs={{0,8},{8,0},{16,24},{24,16},{1,9},{9,1},{17,25},{25,17},{2,10},{10... | collective-permute-start | bytes 147464 | tf_op jit(solution)/shard_map/ppermute | solution.py:17
  27.8 5.2 %collective-permute-start.1 = (f32[6,2048]{1,0:T(8,128)S(1)}, f32[6,2048]{1,0:T(8,128)S(1)}, u32[]{:S(2)}, u32[]{:S(2)}) collective-permute-start(f32[6,2048]{1,0:T(8,128)S(1)} %add.206), channel_id=1, source_target_pairs={{0,16},{8,24},{16,0},{24,8},{1,17},{9,25},{17,1},{25,9},{2,18},{10... | collective-permute-start | bytes 147464 | tf_op jit(solution)/shard_map/ppermute | solution.py:17
  93.8 4.4 %collective-permute-start.2 = (f32[6,2048]{1,0:T(8,128)S(1)}, f32[6,2048]{1,0:T(8,128)S(1)}, u32[]{:S(2)}, u32[]{:S(2)}) collective-permute-start(f32[6,2048]{1,0:T(8,128)S(1)} %reshape.319), channel_id=1, source_target_pairs={{0,8},{8,0},{16,24},{24,16},{1,9},{9,1},{17,25},{25,17},{2,10},{10... | collective-permute-start | bytes 147464 | tf_op jit(solution)/shard_map/ppermute | solution.py:17
  98.2 5.2 %collective-permute-start.3 = (f32[6,2048]{1,0:T(8,128)S(1)}, f32[6,2048]{1,0:T(8,128)S(1)}, u32[]{:S(2)}, u32[]{:S(2)}) collective-permute-start(f32[6,2048]{1,0:T(8,128)S(1)} %add.210), channel_id=1, source_target_pairs={{0,16},{8,24},{16,0},{24,8},{1,17},{9,25},{17,1},{25,9},{2,18},{10... | collective-permute-start | bytes 147464 | tf_op jit(solution)/shard_map/ppermute | solution.py:17
  166.0 4.4 %collective-permute-start.4 = (f32[6,2048]{1,0:T(8,128)S(1)}, f32[6,2048]{1,0:T(8,128)S(1)}, u32[]{:S(2)}, u32[]{:S(2)}) collective-permute-start(f32[6,2048]{1,0:T(8,128)S(1)} %reshape.321), channel_id=1, source_target_pairs={{0,8},{8,0},{16,24},{24,16},{1,9},{9,1},{17,25},{25,17},{2,10},{10... | collective-permute-start | bytes 147464 | tf_op jit(solution)/shard_map/ppermute | solution.py:17
  170.5 5.3 %collective-permute-start.5 = (f32[6,2048]{1,0:T(8,128)S(1)}, f32[6,2048]{1,0:T(8,128)S(1)}, u32[]{:S(2)}, u32[]{:S(2)}) collective-permute-start(f32[6,2048]{1,0:T(8,128)S(1)} %add.216), channel_id=1, source_target_pairs={{0,16},{8,24},{16,0},{24,8},{1,17},{9,25},{17,1},{25,9},{2,18},{10... | collective-permute-start | bytes 147464 | tf_op jit(solution)/shard_map/ppermute | solution.py:17
